TPU v7x, 32 devices: a whole 2x2x4 slice. The times are simulated.
32 devices in a mesh: dp: 2 (over x), mx: 4 (over y, core), my: 4 (over z).
Axes of the slice: x: 2, y: 2, z: 4, core: 2. Of those that a mesh axis runs over, the one named last changes fastest.
Arguments:
- mentor_final_states: bfloat16 [128, 4608], P('dp'), may hold values from -12 to 12
- mentor_output_matrix: bfloat16 [4608, 4096], P(None, ('mx', 'my')), may hold values from -0.09375 to 0.09375
- learner_final_states: bfloat16 [128, 3584], P('dp', 'mx'), may hold values from -12 to 12
- learner_output_matrix: bfloat16 [3584, 4096], P('mx', 'my'), may hold values from -0.09375 to 0.09375
- loss_mask: int32 [128], P('dp'), may hold values 0 or 1
Outputs:
- mismatch_per_piece: float32 [128], P('dp')
- mean_loss: float32 [], replicated
- student_grad: float32 [128, 4096], P('dp', 'my')
All inputs are finite; a program needn't handle non-finite values.
Results may differ from a plain program's by a relative error of at most 0.0003.
Values sent between devices are 32-bit elements.
A program may use at most 64 MiB of HBM per device.

v0:
```python
import jax
import jax.numpy as jnp
from jax import lax
from jax.sharding import PartitionSpec as P

SOFTENING_HEAT = 2.0


def merged(array, axis, combine):
    everything = jax.tree.map(lambda part: lax.all_gather(part, axis), array)
    first = jax.tree.map(lambda part: part[0], everything)

    def lap(k, so_far):
        return combine(so_far, jax.tree.map(lambda part: part[k], everything))

    return lax.fori_loop(1, lax.axis_size(axis), lap, first)


def row_stats(values):
    row_max = jnp.max(values, axis=1)
    row_sum = jnp.sum(jnp.exp(values - row_max[:, None]), axis=1)
    return (row_max, row_sum)


def join_stats(left_stat, right_stat):
    row_max = jnp.maximum(left_stat[0], right_stat[0])
    row_sum = left_stat[1] * jnp.exp(left_stat[0] - row_max) + right_stat[1] * jnp.exp(
        right_stat[0] - row_max
    )
    return (row_max, row_sum)


def shards(
    mentor_final_states,
    mentor_output_matrix,
    learner_final_states,
    learner_output_matrix,
    loss_mask,
):
    groups = lax.axis_size(("mx", "my"))
    piece_cols = mentor_output_matrix.shape[1]
    lexicon_length = piece_cols * groups
    local_tokens = mentor_final_states.shape[0]
    piece_count = local_tokens * lax.axis_size("dp")
    global_multiplier = SOFTENING_HEAT * lexicon_length * piece_count
    mentor_softened_scores = (
        jnp.dot(mentor_final_states, mentor_output_matrix, preferred_element_type=jnp.float32)
        / SOFTENING_HEAT
    )
    learner_contribution = jnp.dot(
        learner_final_states, learner_output_matrix, preferred_element_type=jnp.float32
    )
    piece_importance = loss_mask.astype(jnp.float32)
    usable_count = lax.psum(jnp.sum(piece_importance), "dp")
    learner_softened_scores = lax.psum(learner_contribution, "mx") / SOFTENING_HEAT
    teacher_max, teacher_sum = merged(row_stats(mentor_softened_scores), ("mx", "my"), join_stats)
    student_max, student_sum = merged(row_stats(learner_softened_scores), "my", join_stats)
    mentor_logarithmic_odds = mentor_softened_scores - (teacher_max + jnp.log(teacher_sum))[:, None]
    learner_logarithmic_odds = (
        learner_softened_scores - (student_max + jnp.log(student_sum))[:, None]
    )
    block_cols = learner_logarithmic_odds.shape[1]
    every_teacher = lax.all_gather(mentor_logarithmic_odds, ("mx", "my"), axis=1, tiled=True)
    aligned = lax.dynamic_slice_in_dim(
        every_teacher, lax.axis_index("my") * block_cols, block_cols, 1
    )
    mentor_likelihoods = jnp.exp(aligned)
    disorder_amount = jnp.sum(jnp.exp(every_teacher) * every_teacher, axis=1)
    mixed_expectation = lax.psum(
        jnp.sum(mentor_likelihoods * learner_logarithmic_odds, axis=1), "my"
    )
    mismatch_per_piece = SOFTENING_HEAT * SOFTENING_HEAT * (disorder_amount - mixed_expectation)
    prob_gap = jnp.exp(learner_logarithmic_odds) - mentor_likelihoods
    loss_sum = lax.psum(jnp.sum(piece_importance * mismatch_per_piece), "dp")
    mean_loss = loss_sum / usable_count
    multiplier = piece_importance * global_multiplier / usable_count
    student_grad = prob_gap * multiplier[:, None]
    return (mismatch_per_piece, mean_loss, student_grad)


def solution(mesh):
    placed = (P("dp", None), P(None, ("mx", "my")), P("dp", "mx"), P("mx", "my"), P("dp"))
    return jax.shard_map(
        shards, mesh=mesh, in_specs=placed, out_specs=(P("dp"), P(), P("dp", "my")), check_vma=False
    )
```

profile of v0, /device:TPU:0, one launch (start us, length us, event | category | flops | bytes accessed | tf_op | source)
XLA Modules:
  0.0 117.1 jit_solution(11822539685052594690)
XLA Ops:
  8.0 0.0 all-reduce.9.cloned.1.call-start
  8.1 2.9 %fusion.6 = f32[64,1024]{1,0:T(8,128)} fusion(bf16[64,896]{1,0:T(8,128)(2,1)} %param.11, bf16[896,1024]{1,0:T(8,128)(2,1)} %param.12), kind=kOutput, calls=%fused_computation.29 | convolution fusion | flops 117440512 | bytes 2211840 | tf_op jit(solution)/shard_map/dot_general | solution.py:50
  11.0 0.0 all-gather.6.cloned.1.call-start
  11.1 0.6 fusion.5
  11.7 0.6 dynamic-slice
  13.0 0.2 exponential_reduce_fusion.1
  13.2 0.2 dynamic-update-slice
  13.4 0.2 dynamic-update-slice.1
  13.6 36.0 %all-reduce.4 = (f32[1024]{0:T(1024)S(1)}, f32[1024]{0:T(1024)S(1)}) all-reduce(f32[1024]{0:T(1024)S(1)} %dynamic-update-slice, f32[1024]{0:T(1024)S(1)} %dynamic-update-slice.1), channel_id=2, replica_groups=mesh['dp'=2,'mx'=4,'my'=4] {'mx','my'}, use_global_device_ids=true, to_apply=%add | all-reduce | flops 2048 | bytes 16384
  49.6 0.1 reshape.11
  49.7 0.1 reshape.12
  49.8 0.7 while.34
  50.4 0.7 broadcast_subtract_fusion
  51.1 0.0 all-gather.6.cloned.1.call-update
  51.2 0.6 dynamic-slice.2
  52.4 0.0 all-reduce.9.cloned.1.call-done
  52.4 1.1 multiply_reduce_fusion.1
  53.6 0.2 dynamic-update-slice.2
  53.8 1.2 exponential_reduce_fusion
  55.0 0.2 dynamic-update-slice.3
  55.3 8.3 %all-reduce.5 = (f32[256]{0:T(256)S(1)}, f32[256]{0:T(256)S(1)}) all-reduce(f32[256]{0:T(256)S(1)} %dynamic-update-slice.2, f32[256]{0:T(256)S(1)} %dynamic-update-slice.3), channel_id=4, replica_groups=mesh['dp'=2,'mx'=4,'my'=4] {'my'}, use_global_device_ids=true, to_apply=%add.2 | all-reduce | flops 512 | bytes 4096
  63.6 0.1 reshape.13
  63.7 0.1 reshape.14
  63.8 0.1 while.35
  63.9 21.0 %all-gather.6.cloned.1.call-done = f32[64,4096]{1,0:T(8,128)} async-done(((f32[64,256]{1,0:T(8,128)}), f32[64,4096]{1,0:T(8,128)}) %all-gather.6.cloned.1.call-update) | async-done | bytes 1048592 | tf_op jit(solution)/shard_map/all_gather | solution.py:63
  84.9 1.2 %multiply_reduce_fusion = f32[64]{0:T(128)S(1)} fusion(f32[64,4096]{1,0:T(8,128)} %all-gather.6.cloned.1.call-done, s32[]{:T(128)S(6)} %select_n.25, f32[64,1024]{1,0:T(8,128)} %all-reduce.9.cloned.1.call-done, f32[64]{0:T(128)S(1)} %log_add_fusion), kind=kLoop, calls=%fused_computation.16 | loop fusion | flops 262080 | bytes 524804 | tf_op jit(solution)/shard_map/reduce_sum | solution.py:70
  86.2 10.4 %psum.29 = f32[64]{0:T(128)S(1)} all-reduce(f32[64]{0:T(128)S(1)} %multiply_reduce_fusion), channel_id=1, replica_groups=mesh['dp'=2,'mx'=4,'my'=4] {'my'}, use_global_device_ids=true, to_apply=%region_11.0 | all-reduce | flops 64 | bytes 512 | tf_op jit(solution)/shard_map/psum | solution.py:69
  96.6 1.5 %fusion.4 = f32[64]{0:T(128)S(1)} fusion(f32[64,4096]{1,0:T(8,128)} %all-gather.6.cloned.1.call-done), kind=kLoop, calls=%fused_computation.14 | loop fusion | flops 524224 | bytes 1048832 | tf_op jit(solution)/shard_map/reduce_sum | solution.py:68
  98.0 1.1 convert_reduce_fusion
  99.2 5.5 %all-reduce.6 = (f32[]{:T(128)}, f32[]{:T(128)}) all-reduce(f32[]{:T(128)} %get-tuple-element.274, f32[]{:T(128)} %get-tuple-element.273), channel_id=1, replica_groups=mesh['dp'=2,'mx'=4,'my'=4] {'dp'}, use_global_device_ids=true, to_apply=%region_13.0 | all-reduce | flops 2 | bytes 16 | tf_op jit(solution)/shard_map/psum | solution.py:74
  104.7 0.6 multiply_divide_fusion
  106.7 1.8 %subtract_multiply_fusion = f32[64,1024]{1,0:T(8,128)} fusion(f32[64,4096]{1,0:T(8,128)} %all-gather.6.cloned.1.call-done, s32[]{:T(128)S(6)} %select_n.25, f32[64,1024]{1,0:T(8,128)S(1)} %copy-done.1, f32[64]{0:T(128)S(1)} %multiply_divide_fusion, f32[64]{0:T(128)S(1)} %log_add_fusion), kind=kLoop, calls=%fused_computation.15 | loop fusion | flops 262144 | bytes 786948 | tf_op jit(solution)/shard_map/mul | solution.py:77
  (41 shorter events, 0.6 us)
Async XLA Ops:
  8.0 3.1 %copy-start = (bf16[4608,256]{1,0:T(8,128)(2,1)S(1)}, bf16[4608,256]{1,0:T(8,128)(2,1)}, u32[]{:S(2)}) copy-start(bf16[4608,256]{1,0:T(8,128)(2,1)} %param.10) | copy-start | bytes 7077892
  8.0 3.7 %copy-start.5 = (u32[32]{0:T(128)S(1)}, u32[32]{0:T(128)}, u32[]{:S(2)}) copy-start(u32[32]{0:T(128)} %constant.96) | copy-start | bytes 388
  8.0 3.0 %copy-start.2 = (bf16[64,4608]{1,0:T(8,128)(2,1)S(1)}, bf16[64,4608]{1,0:T(8,128)(2,1)}, u32[]{:S(2)}) copy-start(bf16[64,4608]{1,0:T(8,128)(2,1)} %param.9) | copy-start | bytes 1769476
  8.0 44.4 %all-reduce.9.cloned.1.call-start = ((), (), s32[]{:S(2)}) async-start(), calls=%async_computation.1 | async-start | bytes 524288 | tf_op jit(solution)/shard_map/psum | solution.py:55
  11.0 40.2 %copy-start.4 = (u32[32]{0:T(128)S(1)}, u32[32]{0:T(128)}, u32[]{:S(2)}) copy-start(u32[32]{0:T(128)} %constant.106) | copy-start | bytes 388
  11.0 73.9 %all-gather.6.cloned.1.call-start = ((), (), s32[]{:S(2)}) async-start(), calls=%async_computation | async-start | bytes 1114112 | tf_op jit(solution)/shard_map/all_gather | solution.py:63
  11.1 87.0 %copy-start.3 = (s32[64]{0:T(128)S(1)}, s32[64]{0:T(128)}, u32[]{:S(2)}) copy-start(s32[64]{0:T(128)} %param.13) | copy-start | bytes 772
  52.4 54.3 %copy-start.1 = (f32[64,1024]{1,0:T(8,128)S(1)}, f32[64,1024]{1,0:T(8,128)}, u32[]{:S(2)}) copy-start(f32[64,1024]{1,0:T(8,128)} %all-reduce.9.cloned.1.call-done) | copy-start | bytes 786436
Sparse Core Ops, SparseCore 0:
  11.7 34.9 all-reduce.8
Sparse Core Ops, SparseCore 1:
  51.2 33.6 all-gather.5
where the time goes:
time: 117 us
  blocking collectives  60.3 us (52%)
  waiting for transfers between devices  21.1 us (18%)
  between operations  19.5 us (17%)
  other arithmetic  9.9 us (8%)
  matrix products  3.51 us (3%)
  local copies, waits for them, and re-layouts  2.47 us (2%)
    unnamed x2, blocking collectives  44.3 us
    all_gather x1, waiting for transfers between devices, shards(): lax.all_gather(mentor_logarithmic_odds, ('mx', 'my'), axis=1, tiled=True)  21 us
    psum x1, blocking collectives, shards(): lax.psum(jnp.sum(mentor_likelihoods * learner_logarithmic_odds, axis=1),...  10.4 us
    psum x1, blocking collectives, shards(): loss_sum = lax.psum(jnp.sum(piece_importance * mismatch_per_piece), 'dp')  5.55 us
    dot_general x1, matrix products, shards(): jnp.dot(learner_final_states, learner_output_matrix, preferred_element_ty...  2.89 us
  transfers between devices with their start and end apart: 2, of which 1 were waited for; matrix products, arithmetic and copies ran while one was open for 6% of the time, Pallas kernels for 0%

commit v1 on v0

v1 whole, which is shorter than its diff:
```python
import functools

import jax
import jax.numpy as jnp
from jax import lax
from jax.experimental import pallas as pl
from jax.experimental.pallas import tpu as pltpu
from jax.sharding import PartitionSpec as P

SOFTENING_HEAT = 2.0
CORES = 2
TEACHER_CHUNKS = 4
MESH = pl.DeviceIdType.MESH


def kernel(
    sizes,
    ts_hbm, tw_hbm, ss_hbm, sw_hbm, mask_ref,
    mism_ref, loss_ref, grad_ref,
    ts, tw, ss, sw,
    t_own, t_all, s_all, a_send, own, a_recv, b_send, b_recv,
    st_send, st_all, cnt_all, los_all,
    ld_sem, tt_sem, ag_send, ag_sem, rs_send, rs_sem, bs_send, bs_sem,
    st_ssem, st_rsem, cn_ssem, cn_rsem, lo_ssem, lo_rsem,
):
    n_dp, n_mx, n_my = sizes
    h = n_mx // CORES
    group = n_mx * n_my
    dp, mx, my = lax.axis_index("dp"), lax.axis_index("mx"), lax.axis_index("my")
    yy, cc = mx // CORES, mx % CORES
    me = mx * n_my + my
    partner = {"mx": yy * CORES + (1 - cc)}
    tokens, bc = t_own.shape
    kc = tw.shape[0] // TEACHER_CHUNKS

    def remote(src, dst, ssem, rsem, dev):
        return pltpu.make_async_remote_copy(
            src_ref=src, dst_ref=dst, send_sem=ssem, recv_sem=rsem, device_id=dev, device_id_type=MESH
        )

    loads = [pltpu.make_async_copy(ts_hbm, ts, ld_sem.at[0])]
    for k in range(TEACHER_CHUNKS):
        rows = pl.ds(k * kc, kc)
        loads.append(pltpu.make_async_copy(tw_hbm.at[rows, :], tw.at[rows, :], ld_sem.at[1 + k]))
    base = 1 + TEACHER_CHUNKS
    loads.append(pltpu.make_async_copy(ss_hbm, ss, ld_sem.at[base]))
    for k in range(n_mx):
        r, core = k % h, (1 - cc if k < h else cc)
        block = ((yy + r) % h) * CORES + core
        cols = pl.ds(pl.multiple_of(block * bc, bc), bc)
        loads.append(pltpu.make_async_copy(sw_hbm.at[:, cols], sw.at[k], ld_sem.at[base + 1 + k]))
    for c in loads:
        c.start()

    barrier = pltpu.get_barrier_semaphore()
    for k in range(1, group):
        peer = (me + k) % group
        pl.semaphore_signal(
            barrier, inc=1, device_id={"mx": peer // n_my, "my": peer % n_my}, device_id_type=MESH
        )
    for k in range(1, n_dp):
        pl.semaphore_signal(barrier, inc=1, device_id={"dp": (dp + k) % n_dp}, device_id_type=MESH)

    mask = mask_ref[...].astype(jnp.float32)
    cnt_all[dp] = jnp.broadcast_to(jnp.sum(mask, axis=1, keepdims=True), cnt_all.shape[1:])

    loads[0].wait()
    acc = jnp.zeros((tokens, bc), jnp.float32)
    for k in range(TEACHER_CHUNKS):
        loads[1 + k].wait()
        rows = slice(k * kc, (k + 1) * kc)
        acc += jnp.dot(ts[:, rows], tw[rows, :], preferred_element_type=jnp.float32)
    t_own[...] = acc * (1.0 / SOFTENING_HEAT)

    pl.semaphore_wait(barrier, group - 1 + n_dp - 1)

    swap = remote(t_own, t_all.at[my], tt_sem.at[0], tt_sem.at[1], {"mx": my, "my": mx})

    @pl.when(mx != my)
    def _():
        swap.start()

    @pl.when(mx == my)
    def _():
        t_all[mx] = t_own[...]

    def dp_copies(buf, ssem, rsem):
        return [
            remote(buf.at[dp], buf.at[dp], ssem.at[k], rsem.at[k], {"dp": (dp + k) % n_dp})
            for k in range(1, n_dp)
        ]

    cnt_copies = dp_copies(cnt_all, cn_ssem, cn_rsem)
    for c in cnt_copies:
        c.start()

    loads[base].wait()
    ra = []
    for k in range(n_mx):
        loads[base + 1 + k].wait()
        part = jnp.dot(ss[...], sw[k], preferred_element_type=jnp.float32)
        if k < h:
            a_send[k] = part
            c = remote(a_send.at[k], a_recv.at[k], rs_send.at[k], rs_sem.at[k], partner)
            c.start()
            ra.append(c)
        else:
            own[k - h] = part

    rb = []
    for r in list(range(1, h)) + [0]:
        ra[r].wait_recv()
        if r:
            b_send[r] = own[r] + a_recv[r]
            c = remote(
                b_send.at[r], b_recv.at[r], bs_send.at[r], bs_sem.at[r],
                {"mx": ((yy + r) % h) * CORES + cc},
            )
            c.start()
            rb.append(c)
    total = own[0] + a_recv[0]
    for r, c in enumerate(rb):
        c.wait_recv()
        total = total + b_recv[r + 1]
    s_blk = total * (1.0 / SOFTENING_HEAT)
    s_all[mx] = s_blk

    def gather(buf, which):
        firsts = [remote(buf.at[mx], buf.at[mx], ag_send.at[which, r], ag_sem.at[which, r],
                         {"mx": ((yy + r) % h) * CORES + cc}) for r in range(1, h)]
        pairs = []
        for r in range(h):
            slot = ((yy - r + h) % h) * CORES + cc
            pairs.append(remote(buf.at[slot], buf.at[slot], ag_send.at[which, h + r],
                                ag_sem.at[which, h + r], partner))
        return firsts, pairs

    s_first, s_pair = gather(s_all, 0)
    t_first, t_pair = gather(t_all, 1)
    for c in s_first:
        c.start()
    s_pair[0].start()

    @pl.when(mx != my)
    def _():
        swap.wait_recv()

    for c in t_first:
        c.start()
    t_pair[0].start()

    t_blk = t_all[mx]
    mt = jnp.max(t_blk, axis=1, keepdims=True)
    ms = jnp.max(s_blk, axis=1, keepdims=True)
    td, sd = t_blk - mt, s_blk - ms
    et = jnp.exp(td)
    st = jnp.sum(et, axis=1, keepdims=True)
    sS = jnp.sum(jnp.exp(sd), axis=1, keepdims=True)
    cr = jnp.sum(et * (td - sd), axis=1, keepdims=True)
    lane = lax.broadcasted_iota(jnp.int32, (tokens, 128), 1)
    packed = jnp.where(lane == 0, mt, jnp.where(lane == 1, st, jnp.where(lane == 2, ms, jnp.where(lane == 3, sS, cr))))
    if tokens < 128:
        packed = jnp.concatenate([packed, jnp.zeros((128 - tokens, 128), jnp.float32)], axis=0)
    tile = packed.T[:8, :]
    st_send[...] = tile
    st_all[me] = tile
    st_copies = []
    for k in range(1, group):
        peer = (me + k) % group
        c = remote(st_send, st_all.at[me], st_ssem.at[k], st_rsem.at[k],
                   {"mx": peer // n_my, "my": peer % n_my})
        c.start()
        st_copies.append(c)

    for firsts, pairs in ((s_first, s_pair), (t_first, t_pair)):
        for r, c in enumerate(firsts):
            c.wait_recv()
            pairs[r + 1].start()

    for c in cnt_copies:
        c.wait_recv()
    count = jnp.sum(cnt_all[:, 0:1, :], axis=0)
    for c in st_copies:
        c.wait_recv()
    mts, sts, mss, sss, crs = (st_all[:, i, :] for i in range(5))
    top_t = jnp.max(mts, axis=0, keepdims=True)
    top_s = jnp.max(mss, axis=0, keepdims=True)
    w = jnp.exp(mts - top_t)
    sum_t = jnp.sum(sts * w, axis=0, keepdims=True)
    sum_s = jnp.sum(sss * jnp.exp(mss - top_s), axis=0, keepdims=True)
    d = jnp.sum(w * (crs + sts * ((mts - top_t) - (mss - top_s))), axis=0, keepdims=True)
    log_t, log_s = jnp.log(sum_t), jnp.log(sum_s)
    mism = (SOFTENING_HEAT * SOFTENING_HEAT) * (d / sum_t - log_t + log_s)
    mism = mism[:, :tokens]
    mism_ref[...] = mism
    los_all[dp] = jnp.broadcast_to(jnp.sum(mask * mism, axis=1, keepdims=True), los_all.shape[1:])
    los_copies = dp_copies(los_all, lo_ssem, lo_rsem)
    for c in los_copies:
        c.start()

    multiplier = SOFTENING_HEAT * n_mx * n_my * bc * n_dp * tokens
    mult = mask * multiplier / count[:, :tokens]
    if tokens < 128:
        mult = jnp.concatenate([mult, jnp.zeros((1, 128 - tokens), jnp.float32)], axis=1)
    row = lax.broadcasted_iota(jnp.int32, (128, 128), 0)
    back = jnp.where(row == 0, top_t + log_t, jnp.where(row == 1, top_s + log_s, mult)).T
    lt, ls, mu = back[:tokens, 0:1], back[:tokens, 1:2], back[:tokens, 2:3]

    for c in s_pair + t_pair:
        c.wait_recv()
    for j in range(n_mx):
        grad_ref[:, j * bc:(j + 1) * bc] = (jnp.exp(s_all[j] - ls) - jnp.exp(t_all[j] - lt)) * mu

    for c in los_copies:
        c.wait_recv()
    loss_ref[...] = jnp.sum(los_all[:, 0:1, 0:1], axis=0) / count[:, 0:1]

    @pl.when(mx != my)
    def _():
        swap.wait_send()

    for c in cnt_copies + los_copies + ra + rb + s_first + s_pair + t_first + t_pair + st_copies:
        c.wait_send()


def shards(sizes, ts, tw, ss, sw, mask):
    n_dp, n_mx, n_my = sizes
    tokens, bc = ts.shape[0], tw.shape[1]
    cols = sw.shape[1]
    h = n_mx // CORES
    group = n_mx * n_my
    f32 = jnp.float32
    V, D = pltpu.VMEM, pltpu.SemaphoreType.DMA
    hbm = pl.BlockSpec(memory_space=pltpu.HBM)
    vm = pl.BlockSpec(memory_space=pltpu.VMEM)
    mism, loss, grad = pl.pallas_call(
        functools.partial(kernel, sizes),
        out_shape=(
            jax.ShapeDtypeStruct((1, tokens), f32),
            jax.ShapeDtypeStruct((1, 1), f32),
            jax.ShapeDtypeStruct((tokens, cols), f32),
        ),
        in_specs=[hbm, hbm, hbm, hbm, vm],
        out_specs=(vm, vm, vm),
        scratch_shapes=[
            V(ts.shape, ts.dtype), V(tw.shape, tw.dtype), V(ss.shape, ss.dtype),
            V((n_mx, sw.shape[0], bc), sw.dtype),
            V((tokens, bc), f32), V((n_mx, tokens, bc), f32), V((n_mx, tokens, bc), f32),
            V((h, tokens, bc), f32), V((h, tokens, bc), f32), V((h, tokens, bc), f32),
            V((h, tokens, bc), f32), V((h, tokens, bc), f32),
            V((8, 128), f32), V((group, 8, 128), f32), V((n_dp, 8, 128), f32), V((n_dp, 8, 128), f32),
            D((2 + TEACHER_CHUNKS + n_mx,)), D((2,)),
            D((2, 2 * h)), D((2, 2 * h)), D((h,)), D((h,)), D((h,)), D((h,)),
            D((group,)), D((group,)), D((n_dp,)), D((n_dp,)), D((n_dp,)), D((n_dp,)),
        ],
        compiler_params=pltpu.CompilerParams(
            collective_id=0, has_side_effects=True, vmem_limit_bytes=66_500_000
        ),
    )(ts, tw, ss, sw, mask.reshape(1, tokens))
    return mism.reshape(tokens), loss.reshape(()), grad


def solution(mesh):
    sizes = (mesh.shape["dp"], mesh.shape["mx"], mesh.shape["my"])
    placed = (P("dp", None), P(None, ("mx", "my")), P("dp", "mx"), P("mx", "my"), P("dp"))
    return jax.shard_map(
        functools.partial(shards, sizes), mesh=mesh, in_specs=placed,
        out_specs=(P("dp"), P(), P("dp", "my")), check_vma=False,
    )
```

time: 117 us -> 28 us (0.24)
  blocking collectives: 60.3 us -> 0 us
  Pallas kernels: 0 us -> 22.7 us
  waiting for transfers between devices: 21.1 us -> 0 us
  between operations: 19.5 us -> 2.32 us
  other arithmetic: 9.9 us -> 0 us
  matrix products: 3.51 us -> 0 us
    unnamed x2 -> x0, blocking collectives: 44.3 us -> none
    pallas_call x0 -> x1, Pallas kernels: none -> 22.7 us  [shards(): pl.pallas_call(functools.partial(kernel, sizes), out_shape=(jax.ShapeDtyp...]
    all_gather x1 -> x0, waiting for transfers between devices: 21 us -> none  [shards(): lax.all_gather(mentor_logarithmic_odds, ('mx', 'my'), axis=1, tiled=True)]
    psum x2 -> x0, blocking collectives: 16 us -> none  [the longest x1 10.4 us: shards(): lax.psum(jnp.sum(mentor_likelihoods * learner_logarithmic_odds, axis=1),...]
    reduce_sum x5 -> x0, other arithmetic: 5.16 us -> none  [the longest x1 1.47 us: shards(): disorder_amount = jnp.sum(jnp.exp(every_teacher) * every_teacher, axis=1)]
    dot_general x2 -> x0, matrix products: 3.51 us -> none  [the longest x1 2.89 us: shards(): jnp.dot(learner_final_states, learner_output_matrix, preferred_element_ty...]
    mul x1 -> x0, other arithmetic: 1.77 us -> none  [shards(): student_grad = prob_gap * multiplier[:, None]]
    unnamed x22 -> x2, local copies, waits for them, and re-layouts: 2.16 us -> 2.8 us
  transfers between devices with their start and end apart: 2 -> 0, of which waited for: 1 -> 0; matrix products, arithmetic and copies ran while one was open for 6% -> 0% of each run, Pallas kernels for 0% -> 0%
where the time goes in v1:
time: 28 us; the launch traced here: 27.8 us
  Pallas kernels  22.7 us (81%)
  local copies, waits for them, and re-layouts  2.8 us (10%)
  between operations  2.32 us (8%)
    pallas_call x1, Pallas kernels, shards(): pl.pallas_call(functools.partial(kernel, sizes), out_shape=(jax.ShapeDtyp...  22.7 us
    unnamed x2, local copies, waits for them, and re-layouts  2.8 us

profile of v1, /device:TPU:0, one launch (start us, length us, event | category | flops | bytes accessed | tf_op | source)
XLA Modules:
  0.0 27.8 jit_solution(5375304582666767742)
XLA Ops:
  0.6 22.7 %shard_map.76 = (f32[1,64]{1,0:T(1,128)}, f32[1,1]{1,0:T(1,128)}, f32[64,1024]{1,0:T(8,128)}) custom-call(bf16[64,4608]{1,0:T(8,128)(2,1)} %ts_hbm.1, bf16[4608,256]{1,0:T(8,128)(2,1)} %tw_hbm.1, bf16[64,896]{1,0:T(8,128)(2,1)} %ss_hbm.1, bf16[896,1024]{1,0:T(8,128)(2,1)} %sw_hbm.1, s32[1,64]{1,0:T(1,128)} %bitcast.3), custom_call_target="tpu_custom_call" | custom-call | tf_op jit(solution)/shard_map/pallas_call | solution.py:236
  23.3 1.1 %copy.11 = f32[64]{0:T(128)} copy(f32[64]{0:T(128)} %bitcast.4) | data formatting | bytes 512
  25.0 1.7 %copy.13 = f32[64,1024]{1,0:T(8,128)} copy(f32[64,1024]{1,0:T(8,128)} %get-tuple-element.14) | data formatting | bytes 524288

commit v2 on v1

--- a/solution.py
+++ b/solution.py
@@ -16,7 +16,7 @@
 def kernel(
     sizes,
     ts_hbm, tw_hbm, ss_hbm, sw_hbm, mask_ref,
-    mism_ref, loss_ref, grad_ref,
+    small_ref, grad_ref,
     ts, tw, ss, sw,
     t_own, t_all, s_all, a_send, own, a_recv, b_send, b_recv,
     st_send, st_all, cnt_all, los_all,
@@ -49,7 +49,7 @@
         block = ((yy + r) % h) * CORES + core
         cols = pl.ds(pl.multiple_of(block * bc, bc), bc)
         loads.append(pltpu.make_async_copy(sw_hbm.at[:, cols], sw.at[k], ld_sem.at[base + 1 + k]))
-    for c in loads:
+    for c in loads[:base]:
         c.start()
 
     barrier = pltpu.get_barrier_semaphore()
@@ -68,6 +68,9 @@
     acc = jnp.zeros((tokens, bc), jnp.float32)
     for k in range(TEACHER_CHUNKS):
         loads[1 + k].wait()
+        if k == 1:
+            for c in loads[base:]:
+                c.start()
         rows = slice(k * kc, (k + 1) * kc)
         acc += jnp.dot(ts[:, rows], tw[rows, :], preferred_element_type=jnp.float32)
     t_own[...] = acc * (1.0 / SOFTENING_HEAT)
@@ -192,7 +195,7 @@
     log_t, log_s = jnp.log(sum_t), jnp.log(sum_s)
     mism = (SOFTENING_HEAT * SOFTENING_HEAT) * (d / sum_t - log_t + log_s)
     mism = mism[:, :tokens]
-    mism_ref[...] = mism
+    small_ref[0:1, :tokens] = mism
     los_all[dp] = jnp.broadcast_to(jnp.sum(mask * mism, axis=1, keepdims=True), los_all.shape[1:])
     los_copies = dp_copies(los_all, lo_ssem, lo_rsem)
     for c in los_copies:
@@ -213,7 +216,7 @@
 
     for c in los_copies:
         c.wait_recv()
-    loss_ref[...] = jnp.sum(los_all[:, 0:1, 0:1], axis=0) / count[:, 0:1]
+    small_ref[1:2, :] = jnp.sum(los_all[:, 0:1, :], axis=0) / count
 
     @pl.when(mx != my)
     def _():
@@ -221,6 +224,14 @@
 
     for c in cnt_copies + los_copies + ra + rb + s_first + s_pair + t_first + t_pair + st_copies:
         c.wait_send()
+
+
+def deliver(small_ref, grad_ref, mism_ref, loss_ref, out_ref, sem):
+    copy = pltpu.make_async_copy(grad_ref, out_ref, sem)
+    copy.start()
+    mism_ref[...] = small_ref[0:1, :mism_ref.shape[1]]
+    loss_ref[...] = small_ref[1:2, 0:1]
+    copy.wait()
 
 
 def shards(sizes, ts, tw, ss, sw, mask):
@@ -233,15 +244,14 @@
     V, D = pltpu.VMEM, pltpu.SemaphoreType.DMA
     hbm = pl.BlockSpec(memory_space=pltpu.HBM)
     vm = pl.BlockSpec(memory_space=pltpu.VMEM)
-    mism, loss, grad = pl.pallas_call(
+    small, grad = pl.pallas_call(
         functools.partial(kernel, sizes),
         out_shape=(
-            jax.ShapeDtypeStruct((1, tokens), f32),
-            jax.ShapeDtypeStruct((1, 1), f32),
-            jax.ShapeDtypeStruct((tokens, cols), f32),
+            V((8, max(tokens, 128)), f32),
+            V((tokens, cols), f32),
         ),
         in_specs=[hbm, hbm, hbm, hbm, vm],
-        out_specs=(vm, vm, vm),
+        out_specs=(vm, vm),
         scratch_shapes=[
             V(ts.shape, ts.dtype), V(tw.shape, tw.dtype), V(ss.shape, ss.dtype),
             V((n_mx, sw.shape[0], bc), sw.dtype),
@@ -254,9 +264,24 @@
             D((group,)), D((group,)), D((n_dp,)), D((n_dp,)), D((n_dp,)), D((n_dp,)),
         ],
         compiler_params=pltpu.CompilerParams(
-            collective_id=0, has_side_effects=True, vmem_limit_bytes=66_500_000
+            collective_id=0, has_side_effects=True, vmem_limit_bytes=64_000_000
         ),
     )(ts, tw, ss, sw, mask.reshape(1, tokens))
+    mism, loss, grad = pl.pallas_call(
+        deliver,
+        out_shape=(
+            jax.ShapeDtypeStruct((1, tokens), f32),
+            jax.ShapeDtypeStruct((1, 1), f32),
+            jax.ShapeDtypeStruct((tokens, cols), f32),
+        ),
+        in_specs=[vm, vm],
+        out_specs=(vm, vm, hbm),
+        scratch_shapes=[D],
+        compiler_params=pltpu.CompilerParams(vmem_limit_bytes=16 * 1024 * 1024),
+    )(
+        pltpu.with_memory_space_constraint(small, pltpu.VMEM),
+        pltpu.with_memory_space_constraint(grad, pltpu.VMEM),
+    )
     return mism.reshape(tokens), loss.reshape(()), grad
 
 

time: 28 us -> 24 us (0.86)
  local copies, waits for them, and re-layouts: 2.8 us -> 0 us
  between operations: 2.32 us -> 0.64 us
  Pallas kernels: 22.7 us -> 23.2 us
    unnamed x2 -> x0, local copies, waits for them, and re-layouts: 2.8 us -> none
    pallas_call x1 -> x2, Pallas kernels: 22.7 us -> 23.2 us  [the longest x1 21.9 us: shards(): pl.pallas_call(functools.partial(kernel, sizes), out_shape=(V((8, max(tok...]
where the time goes in v2:
time: 24 us; the launch traced here: 23.8 us
  Pallas kernels  23.2 us (97%)
  between operations  0.64 us (3%)
    pallas_call x1, Pallas kernels, shards(): pl.pallas_call(functools.partial(kernel, sizes), out_shape=(V((8, max(tok...  21.9 us
    pallas_call x1, Pallas kernels, shards(): pl.pallas_call(deliver, out_shape=(jax.ShapeDtypeStruct((1, tokens), f32)...  1.23 us

profile of v2, /device:TPU:0, one launch (start us, length us, event | category | flops | bytes accessed | tf_op | source)
XLA Modules:
  0.0 23.8 jit_solution(4335034556556503927)
XLA Ops:
  0.6 21.9 %shard_map.76 = (f32[8,128]{1,0:T(8,128)S(1)}, f32[64,1024]{1,0:T(8,128)S(1)}) custom-call(bf16[64,4608]{1,0:T(8,128)(2,1)} %ts_hbm.1, bf16[4608,256]{1,0:T(8,128)(2,1)} %tw_hbm.1, bf16[64,896]{1,0:T(8,128)(2,1)} %ss_hbm.1, bf16[896,1024]{1,0:T(8,128)(2,1)} %sw_hbm.1, s32[1,64]{1,0:T(1,128)} %bitcast.3), custom_call_target="tpu_custom_call" | custom-call | tf_op jit(solution)/shard_map/pallas_call | solution.py:247
  22.6 1.2 %shard_map.77 = (f32[1,64]{1,0:T(1,128)}, f32[1,1]{1,0:T(1,128)}, f32[64,1024]{1,0:T(8,128)}) custom-call(f32[8,128]{1,0:T(8,128)S(1)} %get-tuple-element.8.small_ref, f32[64,1024]{1,0:T(8,128)S(1)} %get-tuple-element.9.grad_ref), custom_call_target="tpu_custom_call" | custom-call | tf_op jit(solution)/shard_map/pallas_call | solution.py:270
